TPU v7x, 256 devices: a whole 4x4x8 slice. The times are simulated.
256 devices in a mesh: dp: 32 (over y, x, core), mp: 8 (over z).
Axes of the slice: x: 4, y: 4, z: 8, core: 2. Of those that a mesh axis runs over, the one named last changes fastest.
Arguments:
- ref_hidden: bfloat16 [2048, 2048], P('dp', 'mp'), may hold values from -80 to 80
- proxy_hidden: bfloat16 [2048, 2048], P('dp', 'mp'), may hold values from -80 to 80
- ref_gain: float32 [2048], replicated, may hold values from 0.5 to 1.5
- proxy_gain: float32 [2048], replicated, may hold values from 0.5 to 1.5
- ref_head: bfloat16 [2048, 128256], P(None, ('dp', 'mp')), may hold values from -16 to 16
- proxy_head: bfloat16 [2048, 128256], P(None, ('dp', 'mp')), may hold values from -16 to 16
- token_ids: int32 [2048], P('dp'), may hold values from 0 to 128255
- bucket_ids: int32 [2048], P(('dp', 'mp')), may hold values from 0 to 4095
- domain_of_bucket: int32 [4096], replicated, may hold values from 0 to 21
- prior_weights: float32 [22], replicated, may hold values from 0.01 to 0.1
Outputs:
- ref_loss: float32 [2048], P(('dp', 'mp'))
- proxy_loss: float32 [2048], P(('dp', 'mp'))
- bucket_excess: float32 [4096], P(('dp', 'mp'))
- domain_log_weights: float32 [22], replicated
All inputs are finite; a program needn't handle non-finite values.
Results may differ from a plain program's by a relative error of at most 0.0035.
Values may be sent and summed in bfloat16 or wider, within the bound.
A program may use at most 64 MiB of HBM per device.

v0:
```python
import jax
import jax.numpy as jnp
from jax import lax
from jax.sharding import Mesh
from jax.sharding import PartitionSpec as P

DP_MP = ("dp_0", "dp_1", "dp_2", "mp")
DP = ("dp_0", "dp_1", "dp_2")


def in_one_piece(arrays, axis, dim, along):
    widths = [a.shape[along] for a in arrays]
    both = jnp.concatenate(arrays, axis=along)
    filled = lax.all_gather(both, axis, axis=dim, tiled=True)
    return tuple(jnp.split(filled, [sum(widths[:k]) for k in range(1, len(widths))], axis=along))


def gathered_once(x, axis):
    leaves = jax.tree.leaves(x)
    order = sorted(range(len(leaves)), key=lambda k: -leaves[k].size)
    width = (1, *leaves[order[0]].shape)[-1]
    lines = [
        jnp.pad(leaves[k].reshape(-1), (0, -leaves[k].size % width)).reshape(-1, width)
        for k in order
    ]
    both, at, found = (lax.all_gather(jnp.concatenate(lines), axis), 0, {})
    for k, line in zip(order, lines):
        piece = both[:, at : at + len(line)].reshape(len(both), -1)
        found[k] = piece[:, : leaves[k].size].reshape(-1, *leaves[k].shape)
        at += len(line)
    numbers = iter(range(len(leaves)))
    return jax.tree.map(lambda _: found[next(numbers)], x)


def merged_by_axis(x, axes, combine):
    for axis in axes:
        pieces = gathered_once(x, axis)
        x = jax.tree.map(lambda part: part[0], pieces)
        for k in range(1, lax.axis_size(axis)):
            x = combine(x, jax.tree.map(lambda part: part[k], pieces))
    return x


def over_axes(x, axes):
    for axis in axes:
        x = lax.psum(x, axis)
    return x


def normalize(hidden, gain):
    values = hidden.astype(jnp.float32)
    scale = lax.rsqrt(jnp.mean(values * values, -1, keepdims=True) + 1e-05)
    return (values * scale * gain).astype(jnp.bfloat16)


def row_stats(normed, targets, head, offset):
    logits = jnp.dot(normed, head, preferred_element_type=jnp.float32)
    top = jnp.max(logits, -1)
    total = jnp.sum(jnp.exp(logits - top[:, None]), -1)
    columns = lax.broadcasted_iota(jnp.int32, logits.shape, 1) + offset
    target = jnp.sum(jnp.where(columns == targets[:, None], logits, 0.0), -1)
    return (top, total, target)


def both_stats(norm_ref, norm_proxy, targets, ref_head, proxy_head, offset):
    first = row_stats(norm_ref, targets, ref_head, offset)
    second = row_stats(norm_proxy, targets, proxy_head, offset)
    return tuple((jnp.stack([left, right]) for left, right in zip(first, second)))


def combine_rows(earlier, later):
    top = jnp.maximum(earlier[0], later[0])
    total = earlier[1] * jnp.exp(earlier[0] - top) + later[1] * jnp.exp(later[0] - top)
    return (top, total, earlier[2] + later[2])


def on_device(
    ref_hidden,
    proxy_hidden,
    ref_gain,
    proxy_gain,
    ref_head,
    proxy_head,
    token_ids,
    bucket_ids,
    domain_of_bucket,
    prior_weights,
):
    vocab_dev = ref_head.shape[1]
    device = lax.axis_index(DP_MP)
    offset = device * vocab_dev
    own_rows = bucket_ids.shape[0]
    full_ref, full_proxy = in_one_piece((ref_hidden, proxy_hidden), "mp", 1, 0)
    norm_ref = normalize(full_ref, ref_gain)
    norm_proxy = normalize(full_proxy, proxy_gain)
    piece = (
        *in_one_piece((norm_ref, norm_proxy), DP, 0, 1),
        lax.all_gather(token_ids, DP, axis=0, tiled=True),
    )
    stats = both_stats(piece[0], piece[1], piece[2], ref_head, proxy_head, offset)
    top, total, target = tuple((fresh for fresh in stats))
    first_row = device * own_rows
    whole_top, whole_total, whole_target = merged_by_axis((top, total, target), DP_MP, combine_rows)
    own_top = lax.dynamic_slice_in_dim(whole_top, first_row, own_rows, 1)
    own_total = lax.dynamic_slice_in_dim(whole_total, first_row, own_rows, 1)
    own_target = lax.dynamic_slice_in_dim(whole_target, first_row, own_rows, 1)
    losses = own_top + jnp.log(own_total) - own_target
    excess = jnp.maximum(losses[1] - losses[0], 0.0)
    buckets = domain_of_bucket.shape[0]
    domains = prior_weights.shape[0]
    onehot = (bucket_ids[:, None] == lax.broadcasted_iota(jnp.int32, (1, buckets), 1)).astype(
        jnp.float32
    )
    table = jnp.dot(
        jnp.stack([excess, jnp.ones_like(excess)]),
        onehot,
        precision=lax.Precision.HIGHEST,
        preferred_element_type=jnp.float32,
    )
    domain_hot = (
        domain_of_bucket[:, None] == lax.broadcasted_iota(jnp.int32, (1, domains), 1)
    ).astype(jnp.float32)
    bucket_dev = buckets // lax.axis_size(DP_MP)
    first_bucket = device * bucket_dev
    full_table = over_axes(table, DP_MP)
    domain_totals = jnp.dot(
        full_table, domain_hot, precision=lax.Precision.HIGHEST, preferred_element_type=jnp.float32
    )
    own_table = lax.dynamic_slice_in_dim(full_table, first_bucket, bucket_dev, 1)
    bucket_excess = own_table[0] / jnp.maximum(own_table[1], 1.0)
    domain_excess = domain_totals[0] / jnp.maximum(domain_totals[1], 1.0)
    weights = jax.nn.softmax(jnp.log(prior_weights) + 1.0 * domain_excess)
    domain_log_weights = jnp.log(0.999 * weights + 0.001 / domains)
    return (losses[0], losses[1], bucket_excess, domain_log_weights)


def solution(mesh):
    torus = Mesh(mesh.devices.reshape(4, 4, 2, mesh.shape["mp"]), ("dp_0", "dp_1", "dp_2", "mp"))
    return jax.shard_map(
        on_device,
        mesh=torus,
        in_specs=(
            P(DP, "mp"),
            P(DP, "mp"),
            P(),
            P(),
            P(None, DP_MP),
            P(None, DP_MP),
            P(DP),
            P(DP_MP),
            P(),
            P(),
        ),
        out_specs=(P(DP_MP), P(DP_MP), P(DP_MP), P()),
        check_vma=False,
    )
```

profile of v0, /device:TPU:1, one launch (start us, length us, event | category | flops | bytes accessed | tf_op | source)
XLA Modules:
  0.0 256.5 jit_solution(11383560652746233583)
XLA Ops:
  7.2 0.9 pad_maximum_fusion.1
  8.1 23.7 %all_gather.33 = bf16[128,2048]{1,0:T(8,128)(2,1)S(1)} all-gather(bf16[128,256]{1,0:T(8,128)(2,1)S(1)} %pad_maximum_fusion.1), channel_id=1, replica_groups=mesh['dp_0'=4,'dp_1'=4,'dp_2'=2,'mp'=8] {'mp'}, dimensions={1}, use_global_device_ids=true | all-gather | bytes 589824 | tf_op jit(solution)/shard_map/all_gather | solution.py:14
  32.1 0.9 fusion.8
  33.0 0.8 pad_maximum_fusion
  33.9 1.3 dynamic-slice.1
  35.8 0.9 dynamic-update-slice
  36.7 20.2 %all-reduce.1 = s32[2048]{0:T(1024)S(1)} all-reduce(s32[2048]{0:T(1024)S(1)} %dynamic-update-slice), channel_id=1, replica_groups=mesh['dp_0'=4,'dp_1'=4,'dp_2'=2,'mp'=8] {'dp_0','dp_1','dp_2'}, use_global_device_ids=true, to_apply=%add.1 | all-reduce | flops 2048 | bytes 16384
  56.8 60.5 %all-gather.10.cloned.1.call-done = bf16[2048,4096]{1,0:T(8,128)(2,1)} async-done(((bf16[64,4096]{1,0:T(8,128)(2,1)}), bf16[2048,4096]{1,0:T(8,128)(2,1)}) %all-gather.10.cloned.1.call-update) | async-done | bytes 16777232 | tf_op jit(solution)/shard_map/all_gather | solution.py:14
  117.4 7.1 %fusion.103 = (f32[2048]{0:T(1024)S(1)}, f32[2048,501]{0,1:T(8,128)S(1)}) fusion(bf16[2048,501]{0,1:T(8,128)(2,1)S(1)} %copy-done, bf16[2048,4096]{1,0:T(8,128)(2,1)} %all-gather.10.cloned.1.call-done), kind=kOutput, calls=%fused_computation.188 | convolution fusion | flops 4203716608 | bytes 14553088 | tf_op jit(solution)/shard_map/dot_general | solution.py:57
  124.4 1.2 copy-done.2
  125.6 0.6 copy-done.3
  126.2 4.5 %fusion.104 = (f32[2048]{0:T(1024)S(1)}, f32[2048,501]{0,1:T(8,128)S(1)}) fusion(bf16[2048,501]{0,1:T(8,128)(2,1)S(1)} %copy-done.3, bf16[2048,4096]{1,0:T(8,128)(2,1)S(1)} %copy-done.2), kind=kOutput, calls=%fused_computation.189 | convolution fusion | flops 4203716608 | bytes 14565376 | tf_op jit(solution)/shard_map/dot_general | solution.py:57
  130.7 2.1 fusion.5
  133.0 9.9 %all-gather.4 = f32[4,6,2048]{2,1,0:T(8,128)S(1)} all-gather(f32[1,6,2048]{2,1,0:T(8,128)S(1)} %bitcast.321), channel_id=2, replica_groups=mesh['dp_0'=4,'dp_1'=4,'dp_2'=2,'mp'=8] {'dp_0'}, dimensions={0}, use_global_device_ids=true | all-gather | bytes 245760 | tf_op jit(solution)/shard_map/all_gather | solution.py:26
  143.0 9.4 %all-gather.5 = f32[4,6,2048]{2,1,0:T(8,128)S(1)} all-gather(f32[1,6,2048]{2,1,0:T(8,128)S(1)} %maximum_bitcast_fusion), channel_id=3, replica_groups=mesh['dp_0'=4,'dp_1'=4,'dp_2'=2,'mp'=8] {'dp_1'}, dimensions={0}, use_global_device_ids=true | all-gather | bytes 245760 | tf_op jit(solution)/shard_map/all_gather | solution.py:26
  152.5 7.7 %all-gather.6 = f32[2,6,2048]{2,1,0:T(8,128)S(1)} all-gather(f32[1,6,2048]{2,1,0:T(8,128)S(1)} %maximum_bitcast_fusion.1), channel_id=4, replica_groups=mesh['dp_0'=4,'dp_1'=4,'dp_2'=2,'mp'=8] {'dp_2'}, dimensions={0}, use_global_device_ids=true | all-gather | bytes 147456 | tf_op jit(solution)/shard_map/all_gather | solution.py:26
  160.4 20.8 %all-gather.7 = f32[8,6,2048]{2,1,0:T(8,128)S(1)} all-gather(f32[1,6,2048]{2,1,0:T(8,128)S(1)} %maximum_bitcast_fusion.2), channel_id=5, replica_groups=mesh['dp_0'=4,'dp_1'=4,'dp_2'=2,'mp'=8] {'mp'}, dimensions={0}, use_global_device_ids=true | all-gather | bytes 442368 | tf_op jit(solution)/shard_map/all_gather | solution.py:26
  182.3 12.5 %psum.28 = f32[2,4096]{1,0:T(2,128)S(1)} all-reduce(f32[2,4096]{1,0:T(2,128)S(1)} %fusion.14), channel_id=1, replica_groups=mesh['dp_0'=4,'dp_1'=4,'dp_2'=2,'mp'=8] {'dp_0'}, use_global_device_ids=true, to_apply=%region_8.9 | all-reduce | flops 8192 | bytes 65536 | tf_op jit(solution)/shard_map/psum | solution.py:46
  194.8 11.6 %psum.29 = f32[2,4096]{1,0:T(2,128)S(1)} all-reduce(f32[2,4096]{1,0:T(2,128)S(1)} %psum.28), channel_id=1, replica_groups=mesh['dp_0'=4,'dp_1'=4,'dp_2'=2,'mp'=8] {'dp_1'}, use_global_device_ids=true, to_apply=%region_9.10 | all-reduce | flops 8192 | bytes 65536 | tf_op jit(solution)/shard_map/psum | solution.py:46
  206.5 17.2 %psum.30 = f32[2,4096]{1,0:T(2,128)S(1)} all-reduce(f32[2,4096]{1,0:T(2,128)S(1)} %psum.29), channel_id=1, replica_groups=mesh['dp_0'=4,'dp_1'=4,'dp_2'=2,'mp'=8] {'dp_2'}, use_global_device_ids=true, to_apply=%region_10.11 | all-reduce | flops 8192 | bytes 65536 | tf_op jit(solution)/shard_map/psum | solution.py:46
  223.7 21.2 %psum.31 = f32[2,4096]{1,0:T(2,128)S(1)} all-reduce(f32[2,4096]{1,0:T(2,128)S(1)} %psum.30), channel_id=1, replica_groups=mesh['dp_0'=4,'dp_1'=4,'dp_2'=2,'mp'=8] {'mp'}, use_global_device_ids=true, to_apply=%region_11.12 | all-reduce | flops 8192 | bytes 65536 | tf_op jit(solution)/shard_map/psum | solution.py:46
  245.2 0.6 fusion.95
  245.8 1.3 fusion.92
  247.2 1.9 add_log_fusion
  (35 shorter events, 2.8 us)
Async XLA Ops:
  7.2 110.2 %copy-start = (bf16[2048,501]{0,1:T(8,128)(2,1)S(1)}, bf16[2048,501]{0,1:T(8,128)(2,1)}, u32[]{:S(2)}) copy-start(bf16[2048,501]{0,1:T(8,128)(2,1)} %param.14) | copy-start | bytes 6156292
  7.2 110.2 %all-gather.10.cloned.1.call-start = ((), (), s32[]{:S(2)}) async-start(), calls=%async_computation | async-start | bytes 17301504 | tf_op jit(solution)/shard_map/all_gather | solution.py:14
  117.4 8.2 %copy-start.2 = (bf16[2048,4096]{1,0:T(8,128)(2,1)S(1)}, bf16[2048,4096]{1,0:T(8,128)(2,1)}, u32[]{:S(2)}) copy-start(bf16[2048,4096]{1,0:T(8,128)(2,1)} %all-gather.10.cloned.1.call-done) | copy-start | bytes 50331652
  117.4 8.8 %copy-start.3 = (bf16[2048,501]{0,1:T(8,128)(2,1)S(1)}, bf16[2048,501]{0,1:T(8,128)(2,1)}, u32[]{:S(2)}) copy-start(bf16[2048,501]{0,1:T(8,128)(2,1)} %param.15) | copy-start | bytes 6156292
  130.7 51.4 %copy-start.5 = (s32[8]{0:T(128)S(1)}, s32[8]{0:T(128)}, u32[]{:S(2)}) copy-start(s32[8]{0:T(128)} %param.17) | copy-start | bytes 100
  130.7 114.2 %copy-start.4 = (s32[4096]{0:T(1024)S(1)}, s32[4096]{0:T(1024)}, u32[]{:S(2)}) copy-start(s32[4096]{0:T(1024)} %param.18) | copy-start | bytes 49156
  130.7 114.5 %copy-start.1 = (f32[22]{0:T(128)S(1)}, f32[22]{0:T(128)}, u32[]{:S(2)}) copy-start(f32[22]{0:T(128)} %param.19) | copy-start | bytes 268
Sparse Core Ops, SparseCore 0:
  34.0 83.3 all-gather.9
where the time goes:
time: 262 us; the launch traced here: 256 us
  blocking collectives  154 us (59%)
  waiting for transfers between devices  60.5 us (23%)
  between operations  14.9 us (6%)
  matrix products  12.1 us (5%)
  other arithmetic  10.6 us (4%)
  local copies, waits for them, and re-layouts  4.07 us (2%)
    psum x4, blocking collectives, over_axes(): x = lax.psum(x, axis)  62.6 us
    all_gather x1, waiting for transfers between devices, in_one_piece(): filled = lax.all_gather(both, axis, axis=dim, tiled=True)  60.5 us
    all_gather x4, blocking collectives, gathered_once(): both, at, found = (lax.all_gather(jnp.concatenate(lines), axis), 0, {})  47.7 us
    all_gather x1, blocking collectives, in_one_piece(): filled = lax.all_gather(both, axis, axis=dim, tiled=True)  23.7 us
    unnamed x1, blocking collectives  20.2 us
    dot_general x2, matrix products, row_stats(): logits = jnp.dot(normed, head, preferred_element_type=jnp.float32)  11.6 us
  transfers between devices with their start and end apart: 1, of which 1 were waited for; matrix products, arithmetic and copies ran while one was open for 1% of the time, Pallas kernels for 0%

commit v1 on v0

v1 whole, which is shorter than its diff:
```python
import jax
import jax.numpy as jnp
from jax import lax
from jax.experimental import pallas as pl
from jax.experimental.pallas import tpu as pltpu
from jax.sharding import Mesh
from jax.sharding import PartitionSpec as P

DP_MP = ("dp_0", "dp_1", "dp_2", "mp")
DP = ("dp_0", "dp_1", "dp_2")
MESH = pl.DeviceIdType.MESH
NX, NY, NZ = 4, 4, 8
ROWS, FEAT = 64, 256
D = NZ * FEAT
BUCKETS, DOMAINS = 4096, 22
STEPS = ((1, 0, 0), (-1, 0, 0), (0, 1, 0), (0, -1, 0), (0, 0, 1), (0, 0, -1))
SENDS = (
    0, 256, 512, 768, 1024, 1280, 1664, 1920, 2176, 2432, 2688, 2944,
    7712, 7943, 8288, 8544, 8705, 8967, 9376, 9473, 9888, 10208, 10248, 10504,
    10753, 11143, 11296, 11649, 11800, 12056, 12295, 12673, 12935, 13191, 13441, 13703,
    13848, 14216, 14344, 14744, 14984, 15264, 15362, 15719, 15975, 16231, 16448, 16646,
    17064, 17154, 17505, 17761, 17922, 18279, 18472, 18841, 18946, 19206, 19648, 19960,
    19977, 20455, 20486, 20738, 21160, 21416, 21519, 21880, 22146, 22303, 22681, 22943,
    23046, 23301, 23557, 23813, 24129, 24391, 24579, 24835, 25190, 25442, 25705, 25861,
    26122, 26398, 26627, 26883, 27336, 27592, 27662, 28009, 28231, 28487, 28921, 29183,
    29322, 29561, 29830, 29977, 30401, 30663, 30733, 31077, 31333, 31589, 31810, 32101,
    32261, 32618, 32772, 33123, 33386, 33711, 33803, 34158, 34315, 34564, 35017, 35279,
    35332, 35710, 35853, 36162, 36602, 36862, 36887, 37254, 37390, 37658, 38082, 38342,
    38417, 38765, 38979, 39268, 39491, 39789, 39948, 40317, 40460, 40771, 41130, 41390,
    41491, 41858, 42062, 42328, 42698, 42958, 43024, 43406, 43593, 43871, 44186, 44541,
    44565, 44943, 45281, 45402, 45763, 45982, 46102, 46460, 46669, 46968, 47179, 47494,
    47636, 48010, 48203, 48506, 48770, 49069, 49170, 49425, 49773, 50046, 50314, 50637,
    50832, 50964, 51307, 51583, 51867, 52110, 52255, 52624, 52942, 53028, 53474, 53734,
    53787, 54268, 54348, 54565, 54840, 55173, 55322, 55801, 56008, 56102, 56554, 56814,
    56989, 57339, 57546, 57855, 57995, 58256, 58522, 58879, 59081, 59388, 59568, 59824,
    60063, 60413, 60619, 60926, 61168, 61413, 61598, 61944, 62156, 62461, 62608, 62934,
    63129, 63486, 63695, 63995, 64160, 64493, 64664, 65194, 65469, 65753, 65943, 66204,
    66731, 67066, 67258, 67511, 67717, 68268, 68508, 69031, 69252, 69773, 70043, 70289,
    70787, 71841,
)
PIECES = (
    (0, (0, 12, 1, 3), (21, 25, 26, 27)),
    (0, (4, 8, 13, 15), (28, 30, 30, 30)),
    (0, (2, 5, 9, 11), (31, 31, 35, 35)),
    (1, (15, 8, 5, 9), (33, 34, 36, 37)),
    (0, (6, 14, 10, 7), (37, 38, 40, 41)),
    (1, (3, 0, 1, 12), (38, 40, 42, 44)),
    (1, (10, 13, 11, 7), (46, 46, 47, 48)),
    (1, (14, 6, 2, 4), (48, 49, 50, 51)),
)
DOT_STEPS = 1


def moved(v, d):
    x, y, z = v // 32, v // 8 % 4, v % 8
    dx, dy, dz = STEPS[d]
    return ((x + dx) % NX * 4 + (y + dy) % NY) * 8 + (z + dz) % NZ


def plan():
    sends = [(c // 1536, c // 256 % 6, c // 128 % 2, c % 128) for c in SENDS]
    segments, at, arrived = [], 0, set()

    def need(m, v):
        if (m, v) in arrived:
            return []
        arrived.add((m, v))
        return [(m, v)]

    for m, cols, done in PIECES:
        ends = [*done, done[-1] + DOT_STEPS, done[-1] + 2 * DOT_STEPS]
        own = []
        for p, end in enumerate(ends):
            part = []
            while at < len(sends) and sends[at][0] < end:
                part += need(*sends[at][2:]) + [sends[at]]
                at += 1
            if p < 4:
                for vz in range(NZ):
                    part += need(m, cols[p] * NZ + vz)
            own.append(part)
        segments.append(own)
    assert at == len(sends)
    return segments


SEGMENTS = plan()
COUNTS = [sum(c // 256 % 6 == d for c in SENDS) for d in range(6)]


def pick(i, values):
    out = jnp.int32(values[0])
    for k in range(1, len(values)):
        out = jnp.where(i == k, jnp.int32(values[k]), out)
    return out


def kernel(
    hid0, hid1, gain0, gain1, head0, head1, tokens_in, buckets_in, table_in, prior_in,
    loss0, loss1, bucket_out, domain_out,
    buf, nb, hb, lg, gains, tokens, buckets, table, prior, tid, bid, brow, rows, bfull, st, r1, c1, r2, o3, r3,
    lsem, ssem, rsem, hsem, tsem, bsem, wsem, psem, s1, s2, s3,
):
    y, x, c, z = (lax.axis_index(a) for a in DP_MP)
    hidden, heads = (hid0, hid1), (head0, head1)
    vocab = head0.shape[0]

    def wrap(a, k, n):
        return lax.rem(a + (k + n) % n, n)

    xs = [wrap(x, -k, NX) for k in range(NX)]
    ys = [wrap(y, -k, NY) for k in range(NY)]
    zs = [wrap(z, -k, NZ) for k in range(NZ)]

    def slot(m, v):
        return (m * 16 + ys[v // 8 % 4] * 4 + xs[v // 32]) * 8 + zs[v % 8]

    def col_of(w):
        return ys[w % 4] * 4 + xs[w // 4]

    def at(a, b, cc, k):
        return (wrap(y, b, NY), wrap(x, a, NX), cc, wrap(z, k, NZ))

    other = 1 - c
    partner = (y, x, other, z)
    plane = [(a, b) for a in range(NX) for b in range(NY) if (a, b) != (0, 0)]
    column = list(range(1, NZ))
    me_col = y * 4 + x

    def remote(src, dst, ss, rs, dev):
        return pltpu.make_async_remote_copy(
            src_ref=src, dst_ref=dst, send_sem=ss, recv_sem=rs, device_id=dev, device_id_type=MESH
        )

    own_loads = [
        pltpu.make_async_copy(hidden[m], buf.at[slot(m, 0)], lsem.at[m]) for m in range(2)
    ]
    head_loads = [pltpu.make_async_copy(heads[m], hb.at[m, 0], lsem.at[2 + m]) for m in range(2)]
    small_loads = [
        pltpu.make_async_copy(src, dst, lsem.at[4 + k])
        for k, (src, dst) in enumerate(
            (
                (tokens_in, tokens),
                (buckets_in, buckets),
                (gain0, gains.at[0]),
                (gain1, gains.at[1]),
                (table_in, table),
                (prior_in, prior),
            )
        )
    ]
    for load in own_loads + small_loads:
        load.start()

    peers = [at(0, 0, c, k) for k in column]
    peers += [at(0, 0, other, k) for k in range(NZ)]
    peers += [at(a, b, c, 0) for a, b in plane]
    barrier = pltpu.get_barrier_semaphore()
    for peer in peers:
        pl.semaphore_signal(barrier, inc=1, device_id=peer, device_id_type=MESH)
    pl.semaphore_wait(barrier, len(peers))

    def run(ops):
        for op in ops:
            here = buf.at[slot(*op[-2:])]
            if len(op) == 2:
                m, v = op
                if v == 0:
                    own_loads[m].wait()
                else:
                    pltpu.make_async_copy(here, here, rsem.at[m * 128 + v]).wait()
            else:
                _, d, m, v = op
                dx, dy, dz = STEPS[d]
                there = rsem.at[m * 128 + moved(v, d)]
                remote(here, here, ssem.at[d], there, at(dx, dy, c, dz)).start()

    first = SEGMENTS[0][0]
    early = next(k for k, op in enumerate(first) if len(op) == 4 and op[0] >= 2) - 1
    run(first[:early])

    head_sends = [
        remote(heads[m], hb.at[m, 1], hsem.at[0, m], hsem.at[1, m], partner) for m in range(2)
    ]
    for m in range(2):
        head_sends[m].start()
        head_loads[m].start()
    token_sends = [
        remote(tokens, tid.at[me_col], tsem.at[0, a * 4 + b], tsem.at[1, a * 4 + b], at(a, b, c, 0))
        for a, b in plane
    ]
    bucket_sends = [
        remote(buckets, bid.at[z], bsem.at[0, k], bsem.at[1, k], at(0, 0, c, k)) for k in column
    ]
    for load in small_loads:
        load.wait()
    for copy in token_sends + bucket_sends:
        copy.start()
    tid[me_col] = tokens[...]
    bid[z] = buckets[...]
    st[...] = jnp.zeros(st.shape, jnp.float32)

    run(first[early:])

    for copy in bucket_sends:
        copy.wait()
    lane = lax.broadcasted_iota(jnp.int32, (1, 128), 1)
    packed = jnp.zeros((1, 128), jnp.int32)
    for k in range(NZ):
        wide = jnp.concatenate([bid[k]] * 16, axis=1)
        packed = packed + jnp.where(lane // 8 == k + 8 * lax.rem(x, 2), wide, 0)
    brow[...] = packed
    rows[me_col] = packed
    row_sends = [
        remote(brow, rows.at[me_col], wsem.at[0, a * 4 + b], wsem.at[1, a * 4 + b], at(a, b, c, 0))
        for a, b in plane
    ]
    for copy in row_sends:
        copy.start()
    for copy in token_sends:
        copy.wait()
    for copy in head_sends:
        copy.wait()
    for copy in head_loads:
        copy.wait()

    offset = ((me_col * 2 + c) * NZ + z) * vocab
    offset2 = ((me_col * 2 + other) * NZ + z) * vocab
    number = lax.broadcasted_iota(jnp.int32, (vocab, 4 * ROWS), 0)
    tile_row = lax.broadcasted_iota(jnp.int32, (8, 128), 0)
    tile_lane = lax.broadcasted_iota(jnp.int32, (8, 128), 1)
    cols_by_piece = [[col_of(w) for w in p[1]] for p in PIECES]

    def product(head, rows_):
        return lax.dot_general(
            head, rows_, (((1,), (1,)), ((), ())), preferred_element_type=jnp.float32
        )

    def chosen(i, values):
        out = values[0]
        for k in range(1, len(values)):
            out = jnp.where(i == k, values[k], out)
        return out

    def segment(i, p):
        for k in range(len(PIECES)):
            todo = [] if (k, p) == (0, 0) else SEGMENTS[k][p]

            @pl.when(i == k)
            def _(todo=todo):
                run(todo)

    def piece(i, _):
        m = pick(i, [p[0] for p in PIECES])
        cols = [chosen(i, [cs[k] for cs in cols_by_piece]) for k in range(4)]
        for k in range(4):
            segment(i, k)
            base = (m * 16 + cols[k]) * NZ
            total = jnp.zeros((ROWS, FEAT), jnp.float32)
            for f in range(NZ):
                values = buf[base + f].astype(jnp.float32)
                total = total + values * values
            scale = lax.rsqrt(jnp.sum(total, -1, keepdims=True) * (1.0 / D) + 1e-05)
            for f in range(NZ):
                values = buf[base + f].astype(jnp.float32)
                span = slice(f * FEAT, (f + 1) * FEAT)
                nb[k * ROWS : (k + 1) * ROWS, span] = (values * scale * gains[m, :, span]).astype(
                    jnp.bfloat16
                )
        lg[0] = product(hb[m, 0], nb[...])
        segment(i, 4)
        lg[1] = product(hb[m, 1], nb[...])
        ids = jnp.concatenate([tid[col] for col in cols], axis=1)
        left, right = lg[0], lg[1]
        top = jnp.max(jnp.maximum(left, right), 0, keepdims=True)
        sums = jnp.sum(jnp.exp(left - top) + jnp.exp(right - top), 0, keepdims=True)
        target = jnp.sum(
            jnp.where(number == ids - offset, left, 0.0)
            + jnp.where(number == ids - offset2, right, 0.0),
            0,
            keepdims=True,
        )
        partial = top + jnp.log(sums)
        for k, col in enumerate(cols):
            part = slice(k // 2 * 128, k // 2 * 128 + 128)
            both = jnp.where(tile_row % 2 == 0, partial[:, part], target[:, part])
            half = lax.rem(col, 2)
            mine = jnp.where(half == k % 2, both, pltpu.roll(both, 64, 1))
            keep = (tile_row // 2 == m) & (tile_lane // 64 == half)
            st[col // 2] = jnp.where(keep, mine, st[col // 2])
        segment(i, 5)
        return 0

    lax.fori_loop(0, len(PIECES), piece, 0)

    def merged(tiles):
        top = tiles[0]
        for t in tiles[1:]:
            top = jnp.maximum(top, t)
        total, plain = jnp.exp(tiles[0] - top), tiles[0]
        for t in tiles[1:]:
            total, plain = total + jnp.exp(t - top), plain + t
        return jnp.where(tile_row % 2 == 0, top + jnp.log(total), plain)

    first_sends = [
        remote(st.at[wrap(z, k, NZ)], r1.at[k], s1.at[0, k], s1.at[1, k], at(0, 0, c, k))
        for k in column
    ]
    for copy in first_sends:
        copy.start()
    for copy in row_sends:
        copy.wait()
    for q in range(NZ):
        bfull[c, q] = rows[2 * q] + rows[2 * q + 1]
    swap = remote(bfull.at[c], bfull.at[c], psem.at[0], psem.at[1], partner)
    swap.start()
    for d in range(6):
        sent = buf.at[pl.ds(0, COUNTS[d])]
        pltpu.make_async_copy(sent, sent, ssem.at[d]).wait()
    for k, copy in zip(column, first_sends):
        copy.wait()
    c1[...] = merged([st[z]] + [r1[k] for k in column])

    second_sends = [
        remote(c1, r2.at[a * 4 + b], s2.at[0, a * 4 + b], s2.at[1, a * 4 + b], at(a, b, c, 0))
        for a, b in plane
    ]
    for copy in second_sends:
        copy.start()
    swap.wait()
    bucket_rows = [bfull[j // NZ, j % NZ] for j in range(16)]
    low = lax.broadcasted_iota(jnp.int32, (128, 128), 0)
    high = lax.broadcasted_iota(jnp.int32, (32, 128), 0)
    small = table[...].astype(jnp.float32).astype(jnp.bfloat16)
    domain_rows = []
    for ids in bucket_rows:
        onehot = jnp.where(low == ids % 128, 1.0, 0.0).astype(jnp.bfloat16)
        found = jnp.dot(small, onehot, preferred_element_type=jnp.float32)
        domain_rows.append(
            jnp.sum(jnp.where(high == ids // 128, found, 0.0), 0, keepdims=True).astype(jnp.int32)
        )
    device = (me_col * 2 + c) * NZ + z
    bucket_number = lax.broadcasted_iota(jnp.int32, (16, 128), 0) + device * 16
    domain_number = lax.broadcasted_iota(jnp.int32, (24, 128), 0)
    bucket_hot = [bucket_number == ids for ids in bucket_rows]
    domain_hot = [domain_number == ids for ids in domain_rows]

    def counted(hot):
        total = jnp.zeros(hot[0].shape, jnp.float32)
        for h in hot:
            total = total + jnp.where(h, 1.0, 0.0)
        return jnp.maximum(jnp.sum(total, -1, keepdims=True), 1.0)

    bucket_count, domain_count = counted(bucket_hot), counted(domain_hot)
    for copy in second_sends:
        copy.wait()
    whole = merged([c1[...]] + [r2[a * 4 + b] for a, b in plane])
    low_loss, high_loss = whole[0:1] - whole[1:2], whole[2:3] - whole[3:4]
    o3[...] = jnp.zeros(o3.shape, jnp.float32)
    o3[0:1] = low_loss
    o3[1:2] = high_loss
    o3[2:3] = jnp.maximum(high_loss - low_loss, 0.0)

    place = c * NZ + z
    third_sends = [
        remote(o3, r3.at[place], s3.at[0, k], s3.at[1, k], at(0, 0, c, k)) for k in column
    ] + [
        remote(o3, r3.at[place], s3.at[0, 8 + k], s3.at[1, 8 + k], at(0, 0, other, k))
        for k in range(NZ)
    ]
    for copy in third_sends:
        copy.start()
    r3[place] = o3[...]
    for copy in third_sends:
        copy.wait()

    def summed(hot):
        total = jnp.zeros(hot[0].shape, jnp.float32)
        for j, h in enumerate(hot):
            total = total + jnp.where(h, r3[j, 2:3, :], 0.0)
        return jnp.sum(total, -1, keepdims=True)

    def along(values):
        n = values.shape[0]
        diagonal = lax.broadcasted_iota(jnp.int32, (n, 128), 0) == lax.broadcasted_iota(
            jnp.int32, (n, 128), 1
        )
        return jnp.sum(jnp.where(diagonal, values, 0.0), 0, keepdims=True)

    bucket_out[...] = along(summed(bucket_hot) / bucket_count)[:, :16]
    excess = along(summed(domain_hot) / domain_count)[:, :DOMAINS]
    scores = jnp.log(prior[...]) + 1.0 * excess
    raised = jnp.exp(scores - jnp.max(scores, -1, keepdims=True))
    weights = raised / jnp.sum(raised, -1, keepdims=True)
    domain_out[...] = jnp.log(0.999 * weights + 0.001 / DOMAINS)
    mine = r3[c * NZ + me_col // 2]
    begin = lax.rem(me_col, 2) * 64 + z * 8
    mine = pltpu.roll(mine, lax.rem(128 - begin, 128), 1)
    loss0[...] = mine[0:1, :8]
    loss1[...] = mine[1:2, :8]


def on_device(hid0, hid1, gain0, gain1, head0, head1, tokens, buckets, table, prior):
    vocab = head0.shape[1]
    anywhere = pl.BlockSpec(memory_space=pltpu.HBM)
    inside = pl.BlockSpec(memory_space=pltpu.VMEM)
    dma = pltpu.SemaphoreType.DMA
    f32, bf16, i32 = jnp.float32, jnp.bfloat16, jnp.int32
    outs = pl.pallas_call(
        kernel,
        out_shape=[
            jax.ShapeDtypeStruct((1, 8), f32),
            jax.ShapeDtypeStruct((1, 8), f32),
            jax.ShapeDtypeStruct((1, 16), f32),
            jax.ShapeDtypeStruct((1, DOMAINS), f32),
        ],
        in_specs=[anywhere] * 10,
        out_specs=[inside] * 4,
        scratch_shapes=[
            pltpu.VMEM((2 * 16 * NZ, ROWS, FEAT), bf16),
            pltpu.VMEM((4 * ROWS, D), bf16),
            pltpu.VMEM((2, 2, vocab, D), bf16),
            pltpu.VMEM((2, vocab, 4 * ROWS), f32),
            pltpu.VMEM((2, 1, D), f32),
            pltpu.VMEM((1, ROWS), i32),
            pltpu.VMEM((1, 8), i32),
            pltpu.VMEM((32, 128), i32),
            pltpu.VMEM((1, DOMAINS), f32),
            pltpu.VMEM((16, 1, ROWS), i32),
            pltpu.VMEM((NZ, 1, 8), i32),
            pltpu.VMEM((1, 128), i32),
            pltpu.VMEM((16, 1, 128), i32),
            pltpu.VMEM((2, NZ, 1, 128), i32),
            pltpu.VMEM((NZ, 8, 128), f32),
            pltpu.VMEM((NZ, 8, 128), f32),
            pltpu.VMEM((8, 128), f32),
            pltpu.VMEM((16, 8, 128), f32),
            pltpu.VMEM((8, 128), f32),
            pltpu.VMEM((16, 8, 128), f32),
            dma((10,)),
            dma((6,)),
            dma((256,)),
            dma((2, 2)),
            dma((2, 16)),
            dma((2, 8)),
            dma((2, 16)),
            dma((2,)),
            dma((2, 8)),
            dma((2, 16)),
            dma((2, 16)),
        ],
        compiler_params=pltpu.CompilerParams(
            collective_id=0, has_side_effects=True, vmem_limit_bytes=67_043_328
        ),
    )(
        hid0, hid1, gain0.reshape(1, D), gain1.reshape(1, D), head0.T, head1.T,
        tokens.reshape(1, ROWS), buckets.reshape(1, 8), table.reshape(32, 128),
        prior.reshape(1, DOMAINS),
    )
    return tuple(o.reshape(-1) for o in outs)


def solution(mesh):
    torus = Mesh(mesh.devices.reshape(NY, NX, 2, mesh.shape["mp"]), DP_MP)
    return jax.shard_map(
        on_device,
        mesh=torus,
        in_specs=(
            P(DP, "mp"),
            P(DP, "mp"),
            P(),
            P(),
            P(None, DP_MP),
            P(None, DP_MP),
            P(DP),
            P(DP_MP),
            P(),
            P(),
        ),
        out_specs=(P(DP_MP), P(DP_MP), P(DP_MP), P()),
        check_vma=False,
    )
```

time: 262 us -> 90.1 us (0.34); the launches traced: 256 us -> 90 us
  blocking collectives: 154 us -> 0 us
  Pallas kernels: 0 us -> 84.8 us
  waiting for transfers between devices: 60.5 us -> 0 us
  between operations: 14.9 us -> 0.64 us
  matrix products: 12.1 us -> 0 us
  other arithmetic: 10.6 us -> 0 us
    pallas_call x0 -> x1, Pallas kernels: none -> 84.8 us  [on_device(): pl.pallas_call(kernel, out_shape=[jax.ShapeDtypeStruct((1, 8), f32), jax....]
    all_gather x5 -> x0, blocking collectives: 71.5 us -> none  [the longest x4 47.7 us: gathered_once(): both, at, found = (lax.all_gather(jnp.concatenate(lines), axis), 0, {})]
    psum x4 -> x0, blocking collectives: 62.6 us -> none  [over_axes(): x = lax.psum(x, axis)]
    all_gather x1 -> x0, waiting for transfers between devices: 60.5 us -> none  [in_one_piece(): filled = lax.all_gather(both, axis, axis=dim, tiled=True)]
    unnamed x1 -> x0, blocking collectives: 20.2 us -> none
    dot_general x4 -> x0, matrix products: 12.1 us -> none  [the longest x2 11.6 us: row_stats(): logits = jnp.dot(normed, head, preferred_element_type=jnp.float32)]
    reduce_sum x3 -> x0, other arithmetic: 3.68 us -> none  [the longest x1 2.15 us: row_stats(): target = jnp.sum(jnp.where(columns == targets[:, None], logits, 0.0), -1)]
  transfers between devices with their start and end apart: 1 -> 0, of which waited for: 1 -> 0; matrix products, arithmetic and copies ran while one was open for 1% -> 0% of each run, Pallas kernels for 0% -> 0%
where the time goes in v1:
time: 90.1 us; the launch traced here: 90 us
  Pallas kernels  84.8 us (94%)
  local copies, waits for them, and re-layouts  4.57 us (5%)
    pallas_call x1, Pallas kernels, on_device(): pl.pallas_call(kernel, out_shape=[jax.ShapeDtypeStruct((1, 8), f32), jax....  84.8 us
    unnamed x4, local copies, waits for them, and re-layouts  4.57 us

profile of v1, /device:TPU:1, one launch (start us, length us, event | category | flops | bytes accessed | tf_op | source)
XLA Modules:
  0.0 90.0 jit_solution(13149738250523600371)
XLA Ops:
  0.6 84.8 %shard_map.129 = (f32[1,8]{1,0:T(1,128)}, f32[1,8]{1,0:T(1,128)}, f32[1,16]{1,0:T(1,128)}, f32[1,22]{1,0:T(1,128)}) custom-call(bf16[64,256]{1,0:T(8,128)(2,1)} %hid0.1, bf16[64,256]{1,0:T(8,128)(2,1)} %hid1.1, f32[1,2048]{1,0:T(1,128)} %bitcast.15, f32[1,2048]{1,0:T(1,128)} %bitcast.16, bf16[501,2048]{1,0:T(8,128)(2,1)} %bitcast.12, ...), custom_call_target="tpu_custom_call" | custom-call | tf_op jit(solution)/shard_map/pallas_call | solution.py:409
  85.4 1.1 %copy.18 = f32[8]{0:T(128)} copy(f32[8]{0:T(128)} %bitcast.23) | data formatting | bytes 64
  86.5 1.1 %copy.19 = f32[8]{0:T(128)} copy(f32[8]{0:T(128)} %bitcast.22) | data formatting | bytes 64
  87.7 1.2 %copy.20 = f32[16]{0:T(128)} copy(f32[16]{0:T(128)} %bitcast.21) | data formatting | bytes 128
  88.9 1.1 %copy.21 = f32[22]{0:T(128)} copy(f32[22]{0:T(128)} %bitcast.20) | data formatting | bytes 176

commit v2 on v1

--- a/solution.py
+++ b/solution.py
@@ -13,42 +13,50 @@
 ROWS, FEAT = 64, 256
 D = NZ * FEAT
 BUCKETS, DOMAINS = 4096, 22
-STEPS = ((1, 0, 0), (-1, 0, 0), (0, 1, 0), (0, -1, 0), (0, 0, 1), (0, 0, -1))
+STEPS = ((1, 0, 0), (-1, 0, 0), (0, 1, 0), (0, -1, 0), (0, 0, 1), (0, 0, -1), (0, 0, 2), (0, 0, -2))
+STEPS += tuple(
+    tuple(p + q for p, q in zip(STEPS[a], STEPS[b]))
+    for a in range(6)
+    for b in range(a + 1, 6)
+    if a // 2 != b // 2
+)
+WAYS = len(STEPS)
 SENDS = (
-    0, 256, 512, 768, 1024, 1280, 1664, 1920, 2176, 2432, 2688, 2944,
-    7712, 7943, 8288, 8544, 8705, 8967, 9376, 9473, 9888, 10208, 10248, 10504,
-    10753, 11143, 11296, 11649, 11800, 12056, 12295, 12673, 12935, 13191, 13441, 13703,
-    13848, 14216, 14344, 14744, 14984, 15264, 15362, 15719, 15975, 16231, 16448, 16646,
-    17064, 17154, 17505, 17761, 17922, 18279, 18472, 18841, 18946, 19206, 19648, 19960,
-    19977, 20455, 20486, 20738, 21160, 21416, 21519, 21880, 22146, 22303, 22681, 22943,
-    23046, 23301, 23557, 23813, 24129, 24391, 24579, 24835, 25190, 25442, 25705, 25861,
-    26122, 26398, 26627, 26883, 27336, 27592, 27662, 28009, 28231, 28487, 28921, 29183,
-    29322, 29561, 29830, 29977, 30401, 30663, 30733, 31077, 31333, 31589, 31810, 32101,
-    32261, 32618, 32772, 33123, 33386, 33711, 33803, 34158, 34315, 34564, 35017, 35279,
-    35332, 35710, 35853, 36162, 36602, 36862, 36887, 37254, 37390, 37658, 38082, 38342,
-    38417, 38765, 38979, 39268, 39491, 39789, 39948, 40317, 40460, 40771, 41130, 41390,
-    41491, 41858, 42062, 42328, 42698, 42958, 43024, 43406, 43593, 43871, 44186, 44541,
-    44565, 44943, 45281, 45402, 45763, 45982, 46102, 46460, 46669, 46968, 47179, 47494,
-    47636, 48010, 48203, 48506, 48770, 49069, 49170, 49425, 49773, 50046, 50314, 50637,
-    50832, 50964, 51307, 51583, 51867, 52110, 52255, 52624, 52942, 53028, 53474, 53734,
-    53787, 54268, 54348, 54565, 54840, 55173, 55322, 55801, 56008, 56102, 56554, 56814,
-    56989, 57339, 57546, 57855, 57995, 58256, 58522, 58879, 59081, 59388, 59568, 59824,
-    60063, 60413, 60619, 60926, 61168, 61413, 61598, 61944, 62156, 62461, 62608, 62934,
-    63129, 63486, 63695, 63995, 64160, 64493, 64664, 65194, 65469, 65753, 65943, 66204,
-    66731, 67066, 67258, 67511, 67717, 68268, 68508, 69031, 69252, 69773, 70043, 70289,
-    70787, 71841,
+    0, 256, 512, 768, 1024, 1280, 6656, 6912, 7168, 8448, 12544, 13312,
+    15488, 15744, 16000, 16256, 16512, 16768, 22144, 22400, 30727, 30977, 31233, 31489,
+    31776, 32096, 35872, 36360, 36615, 37128, 40966, 41222, 41474, 41730, 41986, 42246,
+    46082, 46338, 46598, 46854, 47224, 47480, 51256, 51560, 51752, 52088, 52264, 52520,
+    56456, 56800, 57056, 57218, 57400, 57656, 61473, 61799, 61961, 62337, 62568, 62824,
+    66712, 66968, 67208, 67359, 67714, 67992, 71683, 71939, 72197, 72453, 72707, 73062,
+    76805, 77183, 77315, 77695, 77850, 78207, 81934, 82202, 82466, 82722, 83056, 83248,
+    87097, 87310, 87562, 87846, 88112, 88392, 92208, 92518, 92770, 92958, 93249, 93632,
+    97464, 97695, 97984, 98179, 98376, 98719, 102404, 102685, 102947, 103172, 103523, 103693,
+    107549, 107803, 108069, 108414, 108736, 108895, 112698, 112909, 113163, 113443, 113777, 113975,
+    117778, 118027, 118351, 118557, 119032, 119119, 122915, 123249, 123458, 123847, 124136, 124230,
+    128158, 128414, 128712, 128922, 129179, 129438, 133132, 133501, 133644, 134013, 134360, 134525,
+    138285, 138619, 138852, 139131, 139457, 139581, 143414, 143730, 144065, 144187, 144552, 144694,
+    148523, 148836, 149191, 149403, 149753, 149959, 153753, 154011, 154344, 154526, 154857, 155103,
+    158876, 159132, 159465, 159644, 159888, 160254, 163860, 164220, 164520, 164732, 165081, 165352,
+    169117, 169331, 169549, 169887, 170178, 170317, 174234, 174467, 174786, 175005, 175273, 175528,
+    179355, 179585, 179910, 180191, 180355, 180678, 184479, 184827, 185033, 185310, 185578, 185822,
+    189590, 189948, 190121, 190458, 190624, 190854, 194706, 194951, 195311, 195420, 195720, 196079,
+    199828, 200070, 200387, 200666, 200899, 201136, 204947, 205186, 205443, 205757, 205994, 206255,
+    210050, 210326, 210629, 210939, 211171, 211360, 215172, 215444, 215686, 216027, 216299, 216534,
+    220293, 220549, 220807, 221148, 225411, 225924, 226301, 226441, 226798, 230534, 231108, 236165,
+    236715, 236974,
 )
 PIECES = (
-    (0, (0, 12, 1, 3), (21, 25, 26, 27)),
-    (0, (4, 8, 13, 15), (28, 30, 30, 30)),
-    (0, (2, 5, 9, 11), (31, 31, 35, 35)),
-    (1, (15, 8, 5, 9), (33, 34, 36, 37)),
-    (0, (6, 14, 10, 7), (37, 38, 40, 41)),
-    (1, (3, 0, 1, 12), (38, 40, 42, 44)),
-    (1, (10, 13, 11, 7), (46, 46, 47, 48)),
-    (1, (14, 6, 2, 4), (48, 49, 50, 51)),
+    (0, (0, 1, 3, 4), (20, 26, 26, 26)),
+    (0, (12, 2, 5, 15), (26, 32, 32, 32)),
+    (0, (7, 13, 8, 6), (33, 33, 35, 38)),
+    (1, (3, 15, 2, 7), (31, 37, 40, 42)),
+    (0, (11, 14, 9, 10), (38, 38, 39, 44)),
+    (1, (0, 11, 8, 6), (43, 43, 45, 46)),
+    (1, (10, 12, 13, 14), (49, 49, 50, 50)),
+    (1, (4, 9, 1, 5), (51, 51, 52, 52)),
 )
-DOT_STEPS = 1
+DOT_STEPS = 0.5
+AHEAD = 1
 
 
 def moved(v, d):
@@ -58,7 +66,7 @@
 
 
 def plan():
-    sends = [(c // 1536, c // 256 % 6, c // 128 % 2, c % 128) for c in SENDS]
+    sends = [(c // (256 * WAYS), c // 256 % WAYS, c // 128 % 2, c % 128) for c in SENDS]
     segments, at, arrived = [], 0, set()
 
     def need(m, v):
@@ -68,11 +76,11 @@
         return [(m, v)]
 
     for m, cols, done in PIECES:
-        ends = [*done, done[-1] + DOT_STEPS, done[-1] + 2 * DOT_STEPS]
+        ends = [*done, *(done[-1] + DOT_STEPS * (q + 1) for q in range(5))]
         own = []
         for p, end in enumerate(ends):
             part = []
-            while at < len(sends) and sends[at][0] < end:
+            while at < len(sends) and sends[at][0] < end + AHEAD:
                 part += need(*sends[at][2:]) + [sends[at]]
                 at += 1
             if p < 4:
@@ -85,7 +93,7 @@
 
 
 SEGMENTS = plan()
-COUNTS = [sum(c // 256 % 6 == d for c in SENDS) for d in range(6)]
+COUNTS = [sum(c // 256 % WAYS == d for c in SENDS) for d in range(WAYS)]
 
 
 def pick(i, values):
@@ -97,7 +105,7 @@
 
 def kernel(
     hid0, hid1, gain0, gain1, head0, head1, tokens_in, buckets_in, table_in, prior_in,
-    loss0, loss1, bucket_out, domain_out,
+    packed_out,
     buf, nb, hb, lg, gains, tokens, buckets, table, prior, tid, bid, brow, rows, bfull, st, r1, c1, r2, o3, r3,
     lsem, ssem, rsem, hsem, tsem, bsem, wsem, psem, s1, s2, s3,
 ):
@@ -155,6 +163,7 @@
     peers = [at(0, 0, c, k) for k in column]
     peers += [at(0, 0, other, k) for k in range(NZ)]
     peers += [at(a, b, c, 0) for a, b in plane]
+    peers += [at(a, b, c, k) for a, b, k in STEPS if k and (a or b)]
     barrier = pltpu.get_barrier_semaphore()
     for peer in peers:
         pl.semaphore_signal(barrier, inc=1, device_id=peer, device_id_type=MESH)
@@ -267,9 +276,11 @@
                 nb[k * ROWS : (k + 1) * ROWS, span] = (values * scale * gains[m, :, span]).astype(
                     jnp.bfloat16
                 )
-        lg[0] = product(hb[m, 0], nb[...])
-        segment(i, 4)
-        lg[1] = product(hb[m, 1], nb[...])
+        for q in range(4):
+            side, half = q // 2, slice(q % 2 * (D // 2), (q % 2 + 1) * (D // 2))
+            part = product(hb[m, side, :, half], nb[:, half])
+            lg[side] = part if q % 2 == 0 else lg[side] + part
+            segment(i, 4 + q)
         ids = jnp.concatenate([tid[col] for col in cols], axis=1)
         left, right = lg[0], lg[1]
         top = jnp.max(jnp.maximum(left, right), 0, keepdims=True)
@@ -288,7 +299,7 @@
             mine = jnp.where(half == k % 2, both, pltpu.roll(both, 64, 1))
             keep = (tile_row // 2 == m) & (tile_lane // 64 == half)
             st[col // 2] = jnp.where(keep, mine, st[col // 2])
-        segment(i, 5)
+        segment(i, 8)
         return 0
 
     lax.fori_loop(0, len(PIECES), piece, 0)
@@ -314,9 +325,10 @@
         bfull[c, q] = rows[2 * q] + rows[2 * q + 1]
     swap = remote(bfull.at[c], bfull.at[c], psem.at[0], psem.at[1], partner)
     swap.start()
-    for d in range(6):
-        sent = buf.at[pl.ds(0, COUNTS[d])]
-        pltpu.make_async_copy(sent, sent, ssem.at[d]).wait()
+    for d in range(WAYS):
+        if COUNTS[d]:
+            sent = buf.at[pl.ds(0, COUNTS[d])]
+            pltpu.make_async_copy(sent, sent, ssem.at[d]).wait()
     for k, copy in zip(column, first_sends):
         copy.wait()
     c1[...] = merged([st[z]] + [r1[k] for k in column])
@@ -387,17 +399,23 @@
         )
         return jnp.sum(jnp.where(diagonal, values, 0.0), 0, keepdims=True)
 
-    bucket_out[...] = along(summed(bucket_hot) / bucket_count)[:, :16]
+    packed_out[2:3] = along(summed(bucket_hot) / bucket_count)
     excess = along(summed(domain_hot) / domain_count)[:, :DOMAINS]
     scores = jnp.log(prior[...]) + 1.0 * excess
     raised = jnp.exp(scores - jnp.max(scores, -1, keepdims=True))
     weights = raised / jnp.sum(raised, -1, keepdims=True)
-    domain_out[...] = jnp.log(0.999 * weights + 0.001 / DOMAINS)
+    packed_out[3:4, :DOMAINS] = jnp.log(0.999 * weights + 0.001 / DOMAINS)
     mine = r3[c * NZ + me_col // 2]
     begin = lax.rem(me_col, 2) * 64 + z * 8
     mine = pltpu.roll(mine, lax.rem(128 - begin, 128), 1)
-    loss0[...] = mine[0:1, :8]
-    loss1[...] = mine[1:2, :8]
+    packed_out[0:2] = mine[0:2]
+
+
+def unpack(packed, loss0, loss1, bucket_out, domain_out):
+    loss0[...] = packed[0:1, :8]
+    loss1[...] = packed[1:2, :8]
+    bucket_out[...] = packed[2:3, :16]
+    domain_out[...] = packed[3:4, :DOMAINS]
 
 
 def on_device(hid0, hid1, gain0, gain1, head0, head1, tokens, buckets, table, prior):
@@ -406,16 +424,11 @@
     inside = pl.BlockSpec(memory_space=pltpu.VMEM)
     dma = pltpu.SemaphoreType.DMA
     f32, bf16, i32 = jnp.float32, jnp.bfloat16, jnp.int32
-    outs = pl.pallas_call(
+    packed = pl.pallas_call(
         kernel,
-        out_shape=[
-            jax.ShapeDtypeStruct((1, 8), f32),
-            jax.ShapeDtypeStruct((1, 8), f32),
-            jax.ShapeDtypeStruct((1, 16), f32),
-            jax.ShapeDtypeStruct((1, DOMAINS), f32),
-        ],
+        out_shape=jax.ShapeDtypeStruct((8, 128), f32),
         in_specs=[anywhere] * 10,
-        out_specs=[inside] * 4,
+        out_specs=inside,
         scratch_shapes=[
             pltpu.VMEM((2 * 16 * NZ, ROWS, FEAT), bf16),
             pltpu.VMEM((4 * ROWS, D), bf16),
@@ -438,7 +451,7 @@
             pltpu.VMEM((8, 128), f32),
             pltpu.VMEM((16, 8, 128), f32),
             dma((10,)),
-            dma((6,)),
+            dma((WAYS,)),
             dma((256,)),
             dma((2, 2)),
             dma((2, 16)),
@@ -457,6 +470,10 @@
         tokens.reshape(1, ROWS), buckets.reshape(1, 8), table.reshape(32, 128),
         prior.reshape(1, DOMAINS),
     )
+    outs = pl.pallas_call(
+        unpack,
+        out_shape=[jax.ShapeDtypeStruct((1, n), f32) for n in (8, 8, 16, DOMAINS)],
+    )(packed)
     return tuple(o.reshape(-1) for o in outs)
 
 

time: 90.1 us -> 79.8 us (0.89)
  Pallas kernels: 84.8 us -> 79 us
  local copies, waits for them, and re-layouts: 4.57 us -> 0 us
    pallas_call x1 -> x2, Pallas kernels: 84.8 us -> 79 us  [the longest x1 77.8 us: on_device(): pl.pallas_call(kernel, out_shape=jax.ShapeDtypeStruct((8, 128), f32), in_...]
    unnamed x4 -> x0, local copies, waits for them, and re-layouts: 4.57 us -> none
where the time goes in v2:
time: 79.8 us; the launch traced here: 79.7 us
  Pallas kernels  79 us (99%)
    pallas_call x1, Pallas kernels, on_device(): pl.pallas_call(kernel, out_shape=jax.ShapeDtypeStruct((8, 128), f32), in_...  77.8 us

profile of v2, /device:TPU:1, one launch (start us, length us, event | category | flops | bytes accessed | tf_op | source)
XLA Modules:
  0.0 79.7 jit_solution(15656745764397764966)
XLA Ops:
  0.6 77.8 %shard_map.129.packed = f32[8,128]{1,0:T(8,128)} custom-call(bf16[64,256]{1,0:T(8,128)(2,1)} %hid0.1, bf16[64,256]{1,0:T(8,128)(2,1)} %hid1.1, f32[1,2048]{1,0:T(1,128)} %bitcast.15, f32[1,2048]{1,0:T(1,128)} %bitcast.16, bf16[501,2048]{1,0:T(8,128)(2,1)} %bitcast.12, bf16[501,2048]{1,0:T(8,128)(2,1)} %bitcast.13, s32[1,64]{1,0:T(1,128)} %bitcast.17, ...), custom_call_target="tpu_custom_call" | custom-call | tf_op jit(solution)/shard_map/pallas_call | solution.py:427
  78.5 1.2 %shard_map.130 = (f32[1,8]{1,0:T(1,128)}, f32[1,8]{1,0:T(1,128)}, f32[1,16]{1,0:T(1,128)}, f32[1,22]{1,0:T(1,128)}) custom-call(f32[8,128]{1,0:T(8,128)} %shard_map.129.packed), custom_call_target="tpu_custom_call" | custom-call | tf_op jit(solution)/shard_map/pallas_call | solution.py:473

commit v3 on v2

--- a/solution.py
+++ b/solution.py
@@ -132,7 +132,9 @@
     other = 1 - c
     partner = (y, x, other, z)
     plane = [(a, b) for a in range(NX) for b in range(NY) if (a, b) != (0, 0)]
-    column = list(range(1, NZ))
+    plane.sort(key=lambda p: -min(p[0], NX - p[0]) - min(p[1], NY - p[1]))
+    column = sorted(range(1, NZ), key=lambda k: -min(k, NZ - k))
+    whole_column = sorted(range(NZ), key=lambda k: -min(k, NZ - k))
     me_col = y * 4 + x
 
     def remote(src, dst, ss, rs, dev):
@@ -329,16 +331,6 @@
         if COUNTS[d]:
             sent = buf.at[pl.ds(0, COUNTS[d])]
             pltpu.make_async_copy(sent, sent, ssem.at[d]).wait()
-    for k, copy in zip(column, first_sends):
-        copy.wait()
-    c1[...] = merged([st[z]] + [r1[k] for k in column])
-
-    second_sends = [
-        remote(c1, r2.at[a * 4 + b], s2.at[0, a * 4 + b], s2.at[1, a * 4 + b], at(a, b, c, 0))
-        for a, b in plane
-    ]
-    for copy in second_sends:
-        copy.start()
     swap.wait()
     bucket_rows = [bfull[j // NZ, j % NZ] for j in range(16)]
     low = lax.broadcasted_iota(jnp.int32, (128, 128), 0)
@@ -351,6 +343,16 @@
         domain_rows.append(
             jnp.sum(jnp.where(high == ids // 128, found, 0.0), 0, keepdims=True).astype(jnp.int32)
         )
+    for copy in first_sends:
+        copy.wait()
+    c1[...] = merged([st[z]] + [r1[k] for k in column])
+
+    second_sends = [
+        remote(c1, r2.at[a * 4 + b], s2.at[0, a * 4 + b], s2.at[1, a * 4 + b], at(a, b, c, 0))
+        for a, b in plane
+    ]
+    for copy in second_sends:
+        copy.start()
     device = (me_col * 2 + c) * NZ + z
     bucket_number = lax.broadcasted_iota(jnp.int32, (16, 128), 0) + device * 16
     domain_number = lax.broadcasted_iota(jnp.int32, (24, 128), 0)
@@ -378,7 +380,7 @@
         remote(o3, r3.at[place], s3.at[0, k], s3.at[1, k], at(0, 0, c, k)) for k in column
     ] + [
         remote(o3, r3.at[place], s3.at[0, 8 + k], s3.at[1, 8 + k], at(0, 0, other, k))
-        for k in range(NZ)
+        for k in whole_column
     ]
     for copy in third_sends:
         copy.start()

time: 79.8 us -> 79.3 us (level)
  no operation moved by 1% of the time
where the time goes in v3:
time: 79.3 us; the launch traced here: 79.2 us
  Pallas kernels  78.6 us (99%)
    pallas_call x1, Pallas kernels, on_device(): pl.pallas_call(kernel, out_shape=jax.ShapeDtypeStruct((8, 128), f32), in_...  77.4 us

profile of v3, /device:TPU:1, one launch (start us, length us, event | category | flops | bytes accessed | tf_op | source)
XLA Modules:
  0.0 79.2 jit_solution(3918808604352189803)
XLA Ops:
  0.6 77.4 %shard_map.129.packed = f32[8,128]{1,0:T(8,128)} custom-call(bf16[64,256]{1,0:T(8,128)(2,1)} %hid0.1, bf16[64,256]{1,0:T(8,128)(2,1)} %hid1.1, f32[1,2048]{1,0:T(1,128)} %bitcast.15, f32[1,2048]{1,0:T(1,128)} %bitcast.16, bf16[501,2048]{1,0:T(8,128)(2,1)} %bitcast.12, bf16[501,2048]{1,0:T(8,128)(2,1)} %bitcast.13, s32[1,64]{1,0:T(1,128)} %bitcast.17, ...), custom_call_target="tpu_custom_call" | custom-call | tf_op jit(solution)/shard_map/pallas_call | solution.py:429
  78.0 1.2 %shard_map.130 = (f32[1,8]{1,0:T(1,128)}, f32[1,8]{1,0:T(1,128)}, f32[1,16]{1,0:T(1,128)}, f32[1,22]{1,0:T(1,128)}) custom-call(f32[8,128]{1,0:T(8,128)} %shard_map.129.packed), custom_call_target="tpu_custom_call" | custom-call | tf_op jit(solution)/shard_map/pallas_call | solution.py:475
